TPU v7x, 32 devices: a whole 2x2x4 slice. The times are simulated.
32 devices in a mesh: row: 8 (over y, x, core), shift: 4 (over z).
Axes of the slice: x: 2, y: 2, z: 4, core: 2. Of those that a mesh axis runs over, the one named last changes fastest.
Arguments:
- snapshots: bfloat16 [4096, 2, 128], P('row'), may hold values from -6 to 6
- tail_sensors: bfloat16 [128, 2, 128], replicated, may hold values from -6 to 6
- shift_offsets: int32 [12], P('shift'), may hold values from 0 to 128
- start_basis: float32 [64, 4096], P(None, 'row'), may hold values from -0.09375 to 0.09375
Outputs:
- covariance: float32 [4096, 4096], P('row', 'shift')
- signal_basis: float32 [64, 4096], P(None, 'row')
Inputs may be any that keep to these rules, and one draw needn't show every extreme that they name: `shift_offsets`: each shift's first sensor.
All inputs are finite; a program needn't handle non-finite values.
Results may differ from a plain program's by a relative error of at most 0.0031.
Values may be sent and summed in bfloat16 or wider, within the bound.
A program may use at most 64 MiB of HBM per device.

v0:
```python
import jax
import jax.numpy as jnp
from jax import lax
from jax.sharding import PartitionSpec as P

M = 4096
SNAPS = 128
ITERS = 2
half_root = 0.7071067811865476


def make_some(extended, offset, start, count):
    window = lax.dynamic_slice_in_dim(extended, offset + start, count, 0).astype(jnp.float32)
    mirror = lax.dynamic_slice_in_dim(extended, offset + M - start - count, count, 0).astype(
        jnp.float32
    )[::-1]
    summed_pair = window + mirror
    difference = window - mirror
    upper_rows = jnp.concatenate([summed_pair[:, 0], summed_pair[:, 1]], axis=1)
    bottom = jnp.concatenate([difference[:, 1], -difference[:, 0]], axis=1)
    positions = start + jnp.arange(count, dtype=jnp.int32)
    chosen = jnp.where((positions < M // 2)[:, None], upper_rows, bottom)
    return (chosen * half_root).astype(jnp.bfloat16)


def factor(gram_matrix):
    lower_factor = jnp.linalg.cholesky(gram_matrix)
    identity = jnp.eye(gram_matrix.shape[0], dtype=jnp.float32)
    return jax.scipy.linalg.solve_triangular(lower_factor, identity, lower=True)


def per_device(snapshots, tail_sensors, shift_offsets, start_basis):
    block_rows = snapshots.shape[0]
    row_index = lax.axis_index("row")
    shift_index = lax.axis_index("shift")
    col_count = M // lax.axis_size("shift")
    normalizer = 1.0 / (SNAPS * shift_offsets.shape[0] * lax.axis_size("shift"))
    gathered = lax.all_gather(snapshots, "row", axis=0, tiled=True)
    extended = jnp.concatenate([gathered, tail_sensors], 0)
    every_offset = lax.all_gather(shift_offsets, "shift", axis=0, tiled=True)
    row_start = row_index * block_rows
    col_start = shift_index * col_count

    def add_block(which, running):
        offset = every_offset[which]
        own_rows = make_some(extended, offset, row_start, block_rows)
        col_rows = make_some(extended, offset, col_start, col_count)
        return running + lax.dot_general(
            own_rows, col_rows, (((1,), (1,)), ((), ())), preferred_element_type=jnp.float32
        )

    summed_block = lax.fori_loop(
        0, every_offset.shape[0], add_block, jnp.zeros((block_rows, col_count), jnp.float32)
    )
    cov_out = summed_block * normalizer
    basis_rows = lax.all_gather(start_basis, "row", axis=1, tiled=True)
    own_basis = start_basis
    for sweep in range(ITERS):
        basis_cols = lax.dynamic_slice_in_dim(basis_rows, shift_index * col_count, col_count, 1)
        column_terms = lax.dot_general(
            basis_cols, cov_out, (((1,), (1,)), ((), ())), precision=lax.Precision.HIGHEST
        )
        mapped = lax.psum(column_terms, "shift")
        local_gram = jnp.dot(mapped, mapped.T, precision=lax.Precision.HIGHEST)
        gram_matrix = lax.psum(local_gram, "row")
        own_basis = jnp.dot(factor(gram_matrix), mapped, precision=lax.Precision.HIGHEST)
        if sweep + 1 < ITERS:
            basis_rows = lax.all_gather(own_basis, "row", axis=1, tiled=True)
    return (cov_out, own_basis)


def solution(mesh):
    in_specs = (P("row", None, None), P(), P("shift"), P(None, "row"))
    out_specs = (P("row", "shift"), P(None, "row"))
    return jax.shard_map(
        per_device, mesh=mesh, in_specs=in_specs, out_specs=out_specs, check_vma=False
    )
```

profile of v0, /device:TPU:0, one launch (start us, length us, event | category | flops | bytes accessed | tf_op | source)
XLA Modules:
  0.0 375.3 jit_solution(9196168970584460465)
XLA Ops:
  8.7 1.3 dynamic-slice
  11.5 9.9 %all-reduce = s32[12]{0:T(128)S(1)} all-reduce(s32[12]{0:T(128)S(1)} %dynamic-update-slice.2), channel_id=1, replica_groups=mesh['row'=8,'shift'=4] {'shift'}, use_global_device_ids=true, to_apply=%add | all-reduce | flops 12 | bytes 96
  21.4 19.0 %all-gather.4.cloned.1.call-done = bf16[4096,2,128]{2,1,0:T(2,128)(2,1)} async-done(((bf16[512,2,128]{2,1,0:T(2,128)(2,1)}), bf16[4096,2,128]{2,1,0:T(2,128)(2,1)}) %all-gather.4.cloned.1.call-update) | async-done | bytes 2097168 | tf_op jit(solution)/shard_map/all_gather | solution.py:38
  40.4 6.4 %pad_maximum_fusion = bf16[4224,2,128]{2,1,0:T(2,128)(2,1)S(1)} fusion(bf16[128,2,128]{2,1,0:T(2,128)(2,1)} %param.10, bf16[4096,2,128]{2,1,0:T(2,128)(2,1)} %all-gather.4.cloned.1.call-done), kind=kLoop, calls=%fused_computation.31 | loop fusion | flops 1081344 | bytes 4325376 | tf_op jit(solution)/shard_map/concatenate | solution.py:39
  46.8 1.6 copy.30
  48.4 143.1 %while.18 = (s32[]{:T(128)}, f32[512,1024]{1,0:T(8,128)}, s32[]{:T(128)}, s32[12]{0:T(128)S(1)}, bf16[4224,2,128]{2,0,1:T(8,128)(2,1)}, /*index=5*/s32[]{:T(128)...) while((s32[]{:T(128)}, f32[512,1024]{1,0:T(8,128)}, ...), condition=%wide.region_1.2_spmd.clone, body=%wide.region_0.1_spmd.clone.sunk | while | flops 273222688 | bytes 47713820 | solution.py:52
  52.0 1.2 convert_subtract_fusion.4
  59.1 1.3 copy-done.1
  63.9 1.2 convert_subtract_fusion.4
  65.2 1.2 slice_bitcast_fusion.8
  71.0 1.3 copy-done.1
  75.8 1.2 convert_subtract_fusion.4
  77.1 1.2 slice_bitcast_fusion.8
  82.9 1.3 copy-done.1
  87.8 1.2 convert_subtract_fusion.4
  94.9 1.3 copy-done.1
  99.7 1.2 convert_subtract_fusion.4
  106.8 1.3 copy-done.1
  111.6 1.2 convert_subtract_fusion.4
  118.7 1.3 copy-done.1
  123.5 1.2 convert_subtract_fusion.4
  130.6 1.3 copy-done.1
  135.5 1.2 convert_subtract_fusion.4
  142.6 1.3 copy-done.1
  147.4 1.2 convert_subtract_fusion.4
  154.5 1.3 copy-done.1
  159.3 1.2 convert_subtract_fusion.4
  166.4 1.3 copy-done.1
  171.2 1.2 convert_subtract_fusion.4
  178.3 1.3 copy-done.1
  183.2 1.2 convert_subtract_fusion.4
  190.3 1.3 copy-done.1
  191.6 1.8 broadcast_multiply_fusion
  193.4 4.0 %fusion.16 = f32[64,512]{1,0:T(8,128)} fusion(f32[512,1024]{1,0:T(8,128)S(1)} %broadcast_multiply_fusion, f32[64,4096]{1,0:T(8,128)} %all-gather.6.cloned.1.call-done, s32[]{:T(128)S(6)} %select_n.96), kind=kOutput, calls=%fused_computation.35 | convolution fusion | flops 402653184 | bytes 2490372 | tf_op jit(solution)/shard_map/dot_general | solution.py:60
  197.5 34.7 %all-reduce.4.cloned.1.call-done = f32[64,512]{1,0:T(8,128)} async-done(((f32[64,512]{1,0:T(8,128)}), f32[64,512]{1,0:T(8,128)}) %all-reduce.4.cloned.1.call-update) | async-done | bytes 131088 | tf_op jit(solution)/shard_map/psum | solution.py:63
  232.2 1.2 fusion.32
  233.4 22.4 %psum.29 = f32[64,64]{0,1:T(8,128)S(1)} all-reduce(f32[64,64]{0,1:T(8,128)S(1)} %fusion.32), channel_id=1, replica_groups=mesh['row'=8,'shift'=4] {'row'}, use_global_device_ids=true, to_apply=%region_3.4 | all-reduce | flops 4096 | bytes 32768 | tf_op jit(solution)/shard_map/psum | solution.py:65
  255.9 5.8 %cholesky.44 = f32[64,64]{1,0:T(8,128)S(1)} custom-call(f32[64,64]{1,0:T(8,128)S(1)} %fusion.27), custom_call_target="Cholesky" | custom-call | tf_op jit(solution)/shard_map/jit(cholesky)/cholesky | solution.py:27
  263.1 4.9 %custom-call.7 = f32[1,64,64]{1,2,0:T(8,128)S(1)} custom-call(f32[1,64,64]{2,1,0:T(8,128)S(1)} %fusion.22), custom_call_target="InvertDiagBlocksLowerTriangular" | custom-call | tf_op jit(solution)/shard_map/jit(_solve_triangular)/triangular_solve | solution.py:29
  268.2 1.8 fusion.33
  270.1 22.3 %all-gather.8.cloned.1.call-done = f32[64,4096]{1,0:T(8,128)} async-done(((f32[64,512]{1,0:T(8,128)}), f32[64,4096]{1,0:T(8,128)}) %all-gather.8.cloned.1.call-update) | async-done | bytes 1048592 | tf_op jit(solution)/shard_map/all_gather | solution.py:68
  292.4 3.7 fusion.14
  296.2 34.8 %all-reduce.6.cloned.1.call-done = f32[64,512]{1,0:T(8,128)} async-done(((f32[64,512]{1,0:T(8,128)}), f32[64,512]{1,0:T(8,128)}) %all-reduce.6.cloned.1.call-update) | async-done | bytes 131088 | tf_op jit(solution)/shard_map/psum | solution.py:63
  331.0 1.2 fusion.34
  332.2 22.4 %psum.31 = f32[64,64]{0,1:T(8,128)S(1)} all-reduce(f32[64,64]{0,1:T(8,128)S(1)} %fusion.34), channel_id=1, replica_groups=mesh['row'=8,'shift'=4] {'row'}, use_global_device_ids=true, to_apply=%region_7.10 | all-reduce | flops 4096 | bytes 32768 | tf_op jit(solution)/shard_map/psum | solution.py:65
  354.6 5.8 %cholesky.55 = f32[64,64]{1,0:T(8,128)S(1)} custom-call(f32[64,64]{1,0:T(8,128)S(1)} %fusion.25), custom_call_target="Cholesky" | custom-call | tf_op jit(solution)/shard_map/jit(cholesky)/cholesky | solution.py:27
  361.8 4.9 %custom-call.8 = f32[1,64,64]{1,2,0:T(8,128)S(1)} custom-call(f32[1,64,64]{2,1,0:T(8,128)S(1)} %fusion.23), custom_call_target="InvertDiagBlocksLowerTriangular" | custom-call | tf_op jit(solution)/shard_map/jit(_solve_triangular)/triangular_solve | solution.py:29
  367.0 1.8 fusion.35
  (266 shorter events, 89.9 us)
Async XLA Ops:
  7.2 33.2 %all-gather.4.cloned.1.call-start = ((), (), s32[]{:S(2)}) async-start(), calls=%async_computation | async-start | bytes 2359296 | tf_op jit(solution)/shard_map/all_gather | solution.py:38
  7.9 185.5 %all-gather.6.cloned.1.call-start = ((), (), s32[]{:S(2)}) async-start(), calls=%async_computation.1 | async-start | bytes 1179648 | tf_op jit(solution)/shard_map/all_gather | solution.py:56
  8.6 223.5 %all-reduce.4.cloned.1.call-start = ((), (), s32[]{:S(2)}) async-start(), calls=%async_computation.2 | async-start | bytes 262144 | tf_op jit(solution)/shard_map/psum | solution.py:63
  55.7 2.1 copy-start
  56.5 1.4 copy-start.3
  56.5 1.6 copy-start.4
  59.1 1.3 copy-start.1
  67.6 2.1 copy-start
  68.4 1.4 copy-start.3
  68.4 1.6 copy-start.4
  71.0 1.3 copy-start.1
  79.5 2.1 copy-start
  80.4 1.4 copy-start.3
  80.4 1.6 copy-start.4
  82.9 1.3 copy-start.1
  91.5 2.1 copy-start
  92.3 1.4 copy-start.3
  92.3 1.6 copy-start.4
  94.8 1.3 copy-start.1
  103.4 2.1 copy-start
  104.2 1.4 copy-start.3
  104.2 1.6 copy-start.4
  106.8 1.3 copy-start.1
  115.3 2.1 copy-start
  116.1 1.4 copy-start.3
  116.1 1.6 copy-start.4
  118.7 1.3 copy-start.1
  127.2 2.1 copy-start
  128.1 1.4 copy-start.3
  128.1 1.6 copy-start.4
  139.2 2.1 copy-start
  140.0 1.4 copy-start.3
  140.0 1.6 copy-start.4
  151.1 2.1 copy-start
  151.9 1.4 copy-start.3
  151.9 1.6 copy-start.4
  163.0 2.1 copy-start
  163.8 1.4 copy-start.3
  163.8 1.6 copy-start.4
  174.9 2.1 copy-start
  175.8 1.4 copy-start.3
  175.8 1.6 copy-start.4
  186.9 2.1 copy-start
  187.7 1.4 copy-start.3
  187.7 1.6 copy-start.4
  193.4 102.8 %copy-start.5 = (f32[512,1024]{1,0:T(8,128)}, f32[512,1024]{1,0:T(8,128)S(1)}, u32[]{:S(2)}) copy-start(f32[512,1024]{1,0:T(8,128)S(1)} %broadcast_multiply_fusion) | copy-start | bytes 6291460
  197.4 95.0 %all-gather.8.cloned.1.call-start = ((), (), s32[]{:S(2)}) async-start(), calls=%async_computation.3 | async-start | bytes 1179648 | tf_op jit(solution)/shard_map/all_gather | solution.py:68
  270.1 60.9 %all-reduce.6.cloned.1.call-start = ((), (), s32[]{:S(2)}) async-start(), calls=%async_computation.4 | async-start | bytes 262144 | tf_op jit(solution)/shard_map/psum | solution.py:63
  (18 other events, 23.6 us)
Sparse Core Ops, SparseCore 0:
  9.9 30.4 all-gather.3
  42.3 23.3 all-gather.5
  197.5 34.6 all-reduce.3
  270.2 22.1 all-gather.7
  296.3 34.6 all-reduce.5
where the time goes:
time: 378 us; the launch traced here: 375 us
  waiting for transfers between devices  112 us (30%)
  other arithmetic  102 us (27%)
  blocking collectives  54.6 us (14%)
  local copies, waits for them, and re-layouts  39.1 us (10%)
  loops' own time  26.2 us (7%)
  matrix products  26 us (7%)
  between operations  14.5 us (4%)
    psum x2, waiting for transfers between devices, per_device(): mapped = lax.psum(column_terms, 'shift')  69.5 us
    psum x2, blocking collectives, per_device(): gram_matrix = lax.psum(local_gram, 'row')  44.7 us
    sub x24, other arithmetic, make_some(): difference = window - mirror  28.7 us
    another operation x1, loops' own time, per_device(): lax.fori_loop(0, every_offset.shape[0], add_block, jnp.zeros((block_rows,...  26.2 us
    convert_element_type x24, other arithmetic, make_some(): lax.dynamic_slice_in_dim(extended, offset + M - start - count, count, 0)  26 us
    all_gather x1, waiting for transfers between devices, per_device(): basis_rows = lax.all_gather(own_basis, 'row', axis=1, tiled=True)  22.3 us
    while x120, local copies, waits for them, and re-layouts  19.4 us
    all_gather x1, waiting for transfers between devices, per_device(): gathered = lax.all_gather(snapshots, 'row', axis=0, tiled=True)  19 us
  transfers between devices with their start and end apart: 5, of which 4 were waited for; matrix products, arithmetic and copies ran while one was open for 29% of the time, Pallas kernels for 0%

commit v1 on v0

--- a/solution.py
+++ b/solution.py
@@ -62,7 +62,7 @@
         )
         mapped = lax.psum(column_terms, "shift")
         local_gram = jnp.dot(mapped, mapped.T, precision=lax.Precision.HIGHEST)
-        gram_matrix = lax.psum(local_gram, "row")
+        gram_matrix = jnp.sum(lax.all_gather(local_gram, "row"), axis=0)
         own_basis = jnp.dot(factor(gram_matrix), mapped, precision=lax.Precision.HIGHEST)
         if sweep + 1 < ITERS:
             basis_rows = lax.all_gather(own_basis, "row", axis=1, tiled=True)

time: 378 us -> 352 us (0.931)
  blocking collectives: 54.6 us -> 28.6 us
    psum x2 -> x0, blocking collectives: 44.7 us -> none  [per_device(): gram_matrix = lax.psum(local_gram, 'row')]
    all_gather x0 -> x2, blocking collectives: none -> 18.7 us  [per_device(): gram_matrix = jnp.sum(lax.all_gather(local_gram, 'row'), axis=0)]
  transfers between devices with their start and end apart: 5 -> 5, of which waited for: 4 -> 4; matrix products, arithmetic and copies ran while one was open for 29% -> 31% of each run, Pallas kernels for 0% -> 0%
where the time goes in v1:
time: 352 us; the launch traced here: 349 us
  waiting for transfers between devices  112 us (32%)
  other arithmetic  102 us (29%)
  local copies, waits for them, and re-layouts  39.1 us (11%)
  blocking collectives  28.6 us (8%)
  loops' own time  26.2 us (7%)
  matrix products  26 us (7%)
  between operations  14.5 us (4%)
    psum x2, waiting for transfers between devices, per_device(): mapped = lax.psum(column_terms, 'shift')  69.5 us
    sub x24, other arithmetic, make_some(): difference = window - mirror  28.7 us
    another operation x1, loops' own time, per_device(): lax.fori_loop(0, every_offset.shape[0], add_block, jnp.zeros((block_rows,...  26.2 us
    convert_element_type x24, other arithmetic, make_some(): lax.dynamic_slice_in_dim(extended, offset + M - start - count, count, 0)  26 us
    all_gather x1, waiting for transfers between devices, per_device(): basis_rows = lax.all_gather(own_basis, 'row', axis=1, tiled=True)  22.3 us
    while x120, local copies, waits for them, and re-layouts  19.4 us
    all_gather x1, waiting for transfers between devices, per_device(): gathered = lax.all_gather(snapshots, 'row', axis=0, tiled=True)  19 us
    all_gather x2, blocking collectives, per_device(): gram_matrix = jnp.sum(lax.all_gather(local_gram, 'row'), axis=0)  18.7 us
  transfers between devices with their start and end apart: 5, of which 4 were waited for; matrix products, arithmetic and copies ran while one was open for 31% of the time, Pallas kernels for 0%

profile of v1, /device:TPU:0, one launch (start us, length us, event | category | flops | bytes accessed | tf_op | source)
XLA Modules:
  0.0 349.4 jit_solution(7911888086102522323)
XLA Ops:
  8.7 1.3 dynamic-slice
  11.5 9.9 %all-reduce = s32[12]{0:T(128)S(1)} all-reduce(s32[12]{0:T(128)S(1)} %dynamic-update-slice.2), channel_id=1, replica_groups=mesh['row'=8,'shift'=4] {'shift'}, use_global_device_ids=true, to_apply=%add | all-reduce | flops 12 | bytes 96
  21.4 19.0 %all-gather.6.cloned.1.call-done = bf16[4096,2,128]{2,1,0:T(2,128)(2,1)} async-done(((bf16[512,2,128]{2,1,0:T(2,128)(2,1)}), bf16[4096,2,128]{2,1,0:T(2,128)(2,1)}) %all-gather.6.cloned.1.call-update) | async-done | bytes 2097168 | tf_op jit(solution)/shard_map/all_gather | solution.py:38
  40.4 6.4 %pad_maximum_fusion = bf16[4224,2,128]{2,1,0:T(2,128)(2,1)S(1)} fusion(bf16[128,2,128]{2,1,0:T(2,128)(2,1)} %param.10, bf16[4096,2,128]{2,1,0:T(2,128)(2,1)} %all-gather.6.cloned.1.call-done), kind=kLoop, calls=%fused_computation.31 | loop fusion | flops 1081344 | bytes 4325376 | tf_op jit(solution)/shard_map/concatenate | solution.py:39
  46.8 1.6 copy.26
  48.4 143.1 %while.18 = (s32[]{:T(128)}, f32[512,1024]{1,0:T(8,128)}, s32[]{:T(128)}, s32[12]{0:T(128)S(1)}, bf16[4224,2,128]{2,0,1:T(8,128)(2,1)}, /*index=5*/s32[]{:T(128)...) while((s32[]{:T(128)}, f32[512,1024]{1,0:T(8,128)}, ...), condition=%wide.region_1.2_spmd.clone, body=%wide.region_0.1_spmd.clone.sunk | while | flops 273222688 | bytes 47713820 | solution.py:52
  52.0 1.2 convert_subtract_fusion.4
  53.2 1.2 slice_bitcast_fusion.8
  59.1 1.3 copy-done.1
  63.9 1.2 convert_subtract_fusion.4
  71.0 1.3 copy-done.1
  75.8 1.2 convert_subtract_fusion.4
  77.1 1.2 slice_bitcast_fusion.8
  82.9 1.3 copy-done.1
  87.8 1.2 convert_subtract_fusion.4
  94.9 1.3 copy-done.1
  99.7 1.2 convert_subtract_fusion.4
  106.8 1.3 copy-done.1
  111.6 1.2 convert_subtract_fusion.4
  118.7 1.3 copy-done.1
  123.5 1.2 convert_subtract_fusion.4
  130.6 1.3 copy-done.1
  135.5 1.2 convert_subtract_fusion.4
  142.6 1.3 copy-done.1
  147.4 1.2 convert_subtract_fusion.4
  154.5 1.3 copy-done.1
  159.3 1.2 convert_subtract_fusion.4
  166.4 1.3 copy-done.1
  171.2 1.2 convert_subtract_fusion.4
  178.3 1.3 copy-done.1
  183.2 1.2 convert_subtract_fusion.4
  190.3 1.3 copy-done.1
  191.6 1.8 broadcast_multiply_fusion
  193.4 4.0 %fusion.16 = f32[64,512]{1,0:T(8,128)} fusion(f32[512,1024]{1,0:T(8,128)S(1)} %broadcast_multiply_fusion, f32[64,4096]{1,0:T(8,128)} %all-gather.8.cloned.1.call-done, s32[]{:T(128)S(6)} %select_n.96), kind=kOutput, calls=%fused_computation.35 | convolution fusion | flops 402653184 | bytes 2490372 | tf_op jit(solution)/shard_map/dot_general | solution.py:60
  197.5 34.7 %all-reduce.4.cloned.1.call-done = f32[64,512]{1,0:T(8,128)} async-done(((f32[64,512]{1,0:T(8,128)}), f32[64,512]{1,0:T(8,128)}) %all-reduce.4.cloned.1.call-update) | async-done | bytes 131088 | tf_op jit(solution)/shard_map/psum | solution.py:63
  232.2 1.2 fusion.32
  233.4 9.2 %all-gather = f32[512,64]{1,0:T(8,128)S(1)} all-gather(f32[64,64]{1,0:T(8,128)S(1)} %fusion.32), channel_id=2, replica_groups=mesh['row'=8,'shift'=4] {'row'}, dimensions={0}, use_global_device_ids=true | all-gather | bytes 147456 | tf_op jit(solution)/shard_map/all_gather | solution.py:65
  242.8 5.8 %cholesky.44 = f32[64,64]{1,0:T(8,128)S(1)} custom-call(f32[64,64]{1,0:T(8,128)S(1)} %fusion.27), custom_call_target="Cholesky" | custom-call | tf_op jit(solution)/shard_map/jit(cholesky)/cholesky | solution.py:27
  250.0 4.9 %custom-call.7 = f32[1,64,64]{1,2,0:T(8,128)S(1)} custom-call(f32[1,64,64]{2,1,0:T(8,128)S(1)} %fusion.22), custom_call_target="InvertDiagBlocksLowerTriangular" | custom-call | tf_op jit(solution)/shard_map/jit(_solve_triangular)/triangular_solve | solution.py:29
  255.1 1.8 fusion.33
  257.0 22.3 %all-gather.10.cloned.1.call-done = f32[64,4096]{1,0:T(8,128)} async-done(((f32[64,512]{1,0:T(8,128)}), f32[64,4096]{1,0:T(8,128)}) %all-gather.10.cloned.1.call-update) | async-done | bytes 1048592 | tf_op jit(solution)/shard_map/all_gather | solution.py:68
  279.3 3.7 %fusion.14 = f32[64,512]{1,0:T(8,128)} fusion(f32[512,1024]{1,0:T(8,128)S(1)} %broadcast_multiply_fusion, f32[64,4096]{1,0:T(8,128)} %all-gather.10.cloned.1.call-done, s32[]{:T(128)S(6)} %select_n.96), kind=kOutput, calls=%fused_computation.33 | convolution fusion | flops 402653184 | bytes 2490372 | tf_op jit(solution)/shard_map/dot_general | solution.py:60
  283.1 34.8 %all-reduce.6.cloned.1.call-done = f32[64,512]{1,0:T(8,128)} async-done(((f32[64,512]{1,0:T(8,128)}), f32[64,512]{1,0:T(8,128)}) %all-reduce.6.cloned.1.call-update) | async-done | bytes 131088 | tf_op jit(solution)/shard_map/psum | solution.py:63
  317.9 1.2 fusion.34
  319.1 9.4 %all-gather.1 = f32[512,64]{1,0:T(8,128)S(1)} all-gather(f32[64,64]{1,0:T(8,128)S(1)} %fusion.34), channel_id=3, replica_groups=mesh['row'=8,'shift'=4] {'row'}, dimensions={0}, use_global_device_ids=true | all-gather | bytes 147456 | tf_op jit(solution)/shard_map/all_gather | solution.py:65
  328.7 5.8 %cholesky.55 = f32[64,64]{1,0:T(8,128)S(1)} custom-call(f32[64,64]{1,0:T(8,128)S(1)} %fusion.25), custom_call_target="Cholesky" | custom-call | tf_op jit(solution)/shard_map/jit(cholesky)/cholesky | solution.py:27
  335.8 4.9 %custom-call.8 = f32[1,64,64]{1,2,0:T(8,128)S(1)} custom-call(f32[1,64,64]{2,1,0:T(8,128)S(1)} %fusion.23), custom_call_target="InvertDiagBlocksLowerTriangular" | custom-call | tf_op jit(solution)/shard_map/jit(_solve_triangular)/triangular_solve | solution.py:29
  341.0 1.8 fusion.35
  (268 shorter events, 89.9 us)
Async XLA Ops:
  7.2 33.2 %all-gather.6.cloned.1.call-start = ((), (), s32[]{:S(2)}) async-start(), calls=%async_computation | async-start | bytes 2359296 | tf_op jit(solution)/shard_map/all_gather | solution.py:38
  7.9 185.5 %all-gather.8.cloned.1.call-start = ((), (), s32[]{:S(2)}) async-start(), calls=%async_computation.1 | async-start | bytes 1179648 | tf_op jit(solution)/shard_map/all_gather | solution.py:56
  8.6 223.5 %all-reduce.4.cloned.1.call-start = ((), (), s32[]{:S(2)}) async-start(), calls=%async_computation.2 | async-start | bytes 262144 | tf_op jit(solution)/shard_map/psum | solution.py:63
  55.7 2.1 copy-start
  56.5 1.4 copy-start.3
  56.5 1.6 copy-start.4
  59.1 1.3 copy-start.1
  67.6 2.1 copy-start
  68.4 1.4 copy-start.3
  68.4 1.6 copy-start.4
  71.0 1.3 copy-start.1
  79.5 2.1 copy-start
  80.4 1.4 copy-start.3
  80.4 1.6 copy-start.4
  82.9 1.3 copy-start.1
  91.5 2.1 copy-start
  92.3 1.4 copy-start.3
  92.3 1.6 copy-start.4
  94.8 1.3 copy-start.1
  103.4 2.1 copy-start
  104.2 1.4 copy-start.3
  104.2 1.6 copy-start.4
  106.8 1.3 copy-start.1
  115.3 2.1 copy-start
  116.1 1.4 copy-start.3
  116.1 1.6 copy-start.4
  118.7 1.3 copy-start.1
  127.2 2.1 copy-start
  128.1 1.4 copy-start.3
  128.1 1.6 copy-start.4
  139.2 2.1 copy-start
  140.0 1.4 copy-start.3
  140.0 1.6 copy-start.4
  151.1 2.1 copy-start
  151.9 1.4 copy-start.3
  151.9 1.6 copy-start.4
  163.0 2.1 copy-start
  163.8 1.4 copy-start.3
  163.8 1.6 copy-start.4
  174.9 2.1 copy-start
  175.8 1.4 copy-start.3
  175.8 1.6 copy-start.4
  186.9 2.1 copy-start
  187.7 1.4 copy-start.3
  187.7 1.6 copy-start.4
  193.4 85.9 %copy-start.5 = (f32[512,1024]{1,0:T(8,128)}, f32[512,1024]{1,0:T(8,128)S(1)}, u32[]{:S(2)}) copy-start(f32[512,1024]{1,0:T(8,128)S(1)} %broadcast_multiply_fusion) | copy-start | bytes 6291460
  197.4 81.9 %all-gather.10.cloned.1.call-start = ((), (), s32[]{:S(2)}) async-start(), calls=%async_computation.3 | async-start | bytes 1179648 | tf_op jit(solution)/shard_map/all_gather | solution.py:68
  257.0 60.9 %all-reduce.6.cloned.1.call-start = ((), (), s32[]{:S(2)}) async-start(), calls=%async_computation.4 | async-start | bytes 262144 | tf_op jit(solution)/shard_map/psum | solution.py:63
  (18 other events, 23.6 us)
Sparse Core Ops, SparseCore 0:
  9.9 30.4 all-gather.5
  42.3 23.3 all-gather.7
  197.5 34.6 all-reduce.3
  257.1 22.1 all-gather.9
  283.2 34.6 all-reduce.5
